TPU v7x, 32 devices: a whole 2x2x4 slice. The times are simulated.
32 devices in a mesh: dp: 16 (over z, x, core), tensor: 2 (over y).
Axes of the slice: x: 2, y: 2, z: 4, core: 2. Of those that a mesh axis runs over, the one named last changes fastest.
Arguments:
- residual: bfloat16 [4096, 4096], P('dp', 'tensor'), may hold values from -6 to 6
- fresh_qkv: bfloat16 [4096, 3, 2048], P('dp', None, 'tensor'), may hold values from -110 to 110
- active: int32 [4096], P('dp'), may hold values from 0 to 1
- home_slot: int32 [4096], P('dp'), may hold values from 0 to 4095, as said below
- kv_cache: bfloat16 [4096, 2, 16, 2048], P('dp', None, None, 'tensor'), may hold values from -6 to 6
- lengths: int32 [4096], P('dp'), may hold values from 2 to 16
- w_out: bfloat16 [2048, 4096], P('tensor'), may hold values from -0.125 to 0.125
Outputs:
- updated: bfloat16 [4096, 4096], P('dp', 'tensor')
Inputs may be any that keep to these rules, and one draw needn't show every extreme that they name: Each dp group owns the slots 256 * g to 256 * g + 255; home_slot is a permutation. Among the streams of one dp group, at most 16 active streams have slots in the same owning group, and this is reached in every draw.
All inputs are finite; a program needn't handle non-finite values.
Results may differ from a plain program's by a relative error of at most 0.0062.
Values may be sent and summed in bfloat16 or wider, within the bound.
A program may use at most 128 MiB of HBM per device.

v0:
```python
import jax
import jax.numpy as jnp
from jax import lax
from jax.sharding import PartitionSpec as P

HD = 128


def attend_local(fresh_rows, kv_cache, lengths, heads_local):
    streams_here = fresh_rows.shape[0]
    cache_len = kv_cache.shape[2]
    head_size = fresh_rows.shape[1] // (3 * heads_local)
    score_scale = head_size ** (-0.5)
    fresh_split = fresh_rows.reshape(streams_here, 3, heads_local, head_size)
    query = fresh_split[:, 0]
    key_rows = kv_cache[:, 0].reshape(streams_here, cache_len, heads_local, head_size)
    value_rows = kv_cache[:, 1].reshape(streams_here, cache_len, heads_local, head_size)
    scores = (
        jnp.einsum("bhd,blhd->bhl", query, key_rows, preferred_element_type=jnp.float32)
        * score_scale
    )
    positions = jnp.arange(cache_len, dtype=jnp.int32)
    in_cache = positions[None, None, :] < lengths[:, None, None]
    scores = jnp.where(in_cache, scores, jnp.float32(-1e30))
    own_score = (
        jnp.sum(query.astype(jnp.float32) * fresh_split[:, 1].astype(jnp.float32), axis=-1)
        * score_scale
    )
    row_max = jnp.maximum(jnp.max(scores, axis=-1), own_score)
    weights_raw = jnp.exp(scores - row_max[..., None])
    own_raw = jnp.exp(own_score - row_max)
    denominator = jnp.sum(weights_raw, axis=-1) + own_raw
    weights = (weights_raw / denominator[..., None]).astype(jnp.bfloat16)
    own_weight = (own_raw / denominator).astype(jnp.bfloat16)
    mixed = jnp.einsum("bhl,blhd->bhd", weights, value_rows, preferred_element_type=jnp.float32)
    mixed = mixed + own_weight.astype(jnp.float32)[..., None] * fresh_split[:, 2].astype(
        jnp.float32
    )
    return mixed.astype(jnp.bfloat16).reshape(streams_here, heads_local * head_size)


def body(residual, fresh_qkv, active, home_slot, kv_cache, lengths, w_out):
    groups = lax.axis_size("dp")
    group_here = lax.axis_index("dp")
    streams_here = home_slot.shape[0]
    width_here = fresh_qkv.shape[2]
    heads_local = width_here // HD
    capacity = max(2, streams_here // groups)
    slot_count = groups * capacity
    owner_group = home_slot // streams_here
    is_active = active > 0
    earlier = jnp.arange(streams_here)[:, None] < jnp.arange(streams_here)[None, :]
    same_owner = (
        (owner_group[:, None] == owner_group[None, :])
        & is_active[:, None]
        & is_active[None, :]
        & earlier
    )
    send_rank = jnp.sum(same_owner.astype(jnp.int32), axis=0)
    target = owner_group * capacity + send_rank
    placed = (jnp.arange(slot_count, dtype=jnp.int32)[:, None] == target[None, :]) & is_active[
        None, :
    ]
    placing = placed.astype(jnp.bfloat16)
    fresh_flat = fresh_qkv.reshape(streams_here, 3 * width_here)
    send_rows = jnp.dot(placing, fresh_flat, preferred_element_type=jnp.float32).astype(
        jnp.bfloat16
    )
    send_rows = send_rows.reshape(groups, capacity, 3 * width_here)
    slot_ids = jnp.sum(jnp.where(placed, home_slot[None, :] + 1, 0), axis=1) - 1
    slot_ids = slot_ids.reshape(groups, capacity)
    got_rows, got_ids = (
        lax.all_to_all(send_rows, "dp", split_axis=0, concat_axis=0, tiled=True),
        lax.all_to_all(slot_ids, "dp", split_axis=0, concat_axis=0, tiled=True),
    )
    local_slot = got_ids.reshape(slot_count) - group_here * streams_here
    matched = (local_slot[None, :] == jnp.arange(streams_here, dtype=jnp.int32)[:, None]).astype(
        jnp.bfloat16
    )
    owned = jnp.dot(
        matched, got_rows.reshape(slot_count, 3 * width_here), preferred_element_type=jnp.float32
    ).astype(jnp.bfloat16)
    attended = attend_local(owned, kv_cache, lengths, heads_local)
    heads_rows = jnp.dot(matched.T, attended, preferred_element_type=jnp.float32).astype(
        jnp.bfloat16
    )
    returned = lax.all_to_all(
        heads_rows.reshape(groups, capacity, width_here),
        "dp",
        split_axis=0,
        concat_axis=0,
        tiled=True,
    )
    source_rows = jnp.dot(
        placing.T, returned.reshape(slot_count, width_here), preferred_element_type=jnp.float32
    ).astype(jnp.bfloat16)
    partial_rows = jnp.dot(source_rows, w_out, preferred_element_type=jnp.float32)
    gained = lax.psum_scatter(partial_rows, "tensor", scatter_dimension=1, tiled=True)
    return (residual.astype(jnp.float32) + gained).astype(jnp.bfloat16)


def solution(mesh):
    placed = (
        P("dp", "tensor"),
        P("dp", None, "tensor"),
        P("dp"),
        P("dp"),
        P("dp", None, None, "tensor"),
        P("dp"),
        P("tensor", None),
    )
    return jax.shard_map(
        body, mesh=mesh, in_specs=placed, out_specs=P("dp", "tensor"), check_vma=False
    )
```

profile of v0, /device:TPU:0, one launch (start us, length us, event | category | flops | bytes accessed | tf_op | source)
XLA Modules:
  0.0 170.8 jit_solution(18366352465075356929)
XLA Ops:
  6.5 0.7 broadcast_add_fusion.1
  7.2 0.7 broadcast_compare_fusion
  7.9 0.2 convert_reduce_fusion
  8.1 0.1 select_reduce_fusion
  8.2 0.7 sub.45
  8.9 7.4 %all-to-all-start = ((s32[16,1,16]{2,1,0:T(1,128)}), s32[16,1,16]{2,1,0:T(1,128)S(1)}, u32[]{:S(2)}, u32[]{:S(2)}) async-start(s32[16,1,16]{2,1,0:T(1,128)} %sub.45), calls=%async_computation | async-start | bytes 16384 | tf_op jit(solution)/shard_map/all_to_all | solution.py:74
  16.3 1.7 copy.14
  18.0 1.8 %convolution_convert_fusion.1 = bf16[256,3072]{1,0:T(8,128)(2,1)} fusion(bf16[256,3072]{0,1:T(8,128)(2,1)S(1)} %bitcast.71, s32[256]{0:T(256)S(1)} %multiply_add_fusion, pred[256]{0:T(512)(128)(4,1)S(1)} %broadcast_compare_fusion), kind=kOutput, calls=%fused_computation.5 | convolution fusion | flops 403570688 | bytes 3147008 | tf_op jit(solution)/shard_map/dot_general | solution.py:66
  19.9 2.8 %all-to-all-done = s32[16,1,16]{2,1,0:T(1,128)S(1)} async-done(((s32[16,1,16]{2,1,0:T(1,128)}), s32[16,1,16]{2,1,0:T(1,128)S(1)}, u32[]{:S(2)}, u32[]{:S(2)}) %all-to-all-start) | async-done | bytes 1056 | tf_op jit(solution)/shard_map/all_to_all | solution.py:74
  22.7 3.7 %all-to-all-start.1 = ((bf16[16,16,3072]{2,1,0:T(8,128)(2,1)}), bf16[16,16,3072]{2,1,0:T(8,128)(2,1)S(1)}, u32[]{:S(2)}, u32[]{:S(2)}) async-start(bf16[16,16,3072]{2,1,0:T(8,128)(2,1)} %bitcast.1), calls=%async_computation.1 | async-start | bytes 3145728 | tf_op jit(solution)/shard_map/all_to_all | solution.py:73
  26.4 0.0 reduce-scatter.2.cloned.1.call-start
  26.4 12.4 %fusion.31 = (bf16[256,1,16,1024]{3,2,1,0:T(8,128)(2,1)}, bf16[256,1,16,1024]{3,2,1,0:T(8,128)(2,1)}) fusion(bf16[256,2,16,1024]{3,2,1,0:T(8,128)(2,1)} %param.11), kind=kLoop, calls=%fused_computation.57 | loop fusion | bytes 33554432 | tf_op jit(solution)/shard_map/slice | solution.py:17
  38.8 8.8 %copy.28 = bf16[512,8,8,128]{3,2,1,0:T(8,128)(2,1)} copy(bf16[512,8,8,128]{3,1,2,0:T(8,128)(2,1)} %bitcast.64) | data formatting | bytes 16777216
  47.6 0.0 copy-start.1
  47.6 8.8 %copy.29 = bf16[512,8,8,128]{3,2,1,0:T(8,128)(2,1)} copy(bf16[512,8,8,128]{3,1,2,0:T(8,128)(2,1)} %bitcast.63) | data formatting | bytes 16777216
  56.4 0.0 copy-done.1
  56.4 0.1 sub.48
  56.5 1.6 all-to-all-done.1
  58.2 0.6 fusion.4
  58.8 0.3 copy.27
  59.1 0.3 fusion.8
  59.5 0.1 copy.17
  59.5 7.8 %fusion.2 = f32[256,8,1,16]{3,2,1,0:T(1,128)S(1)} fusion(bf16[256,16,8,128]{3,2,1,0:T(8,128)(2,1)} %bitcast.69, bf16[256,8,128,1]{2,1,0,3:T(8,128)(2,1)S(1)} %slice_bitcast_fusion.2), kind=kOutput, calls=%fused_computation.2 | convolution fusion | flops 8388608 | bytes 9043968 | tf_op jit(solution)/shard_map/bhd,blhd->bhl/dot_general | solution.py:19
  67.3 0.8 copy.21
  68.3 1.1 copy.22
  69.4 0.1 copy.18
  69.6 5.7 %fusion = f32[256,8,1,128]{3,2,1,0:T(1,128)S(1)} fusion(bf16[256,8,16,1]{2,3,1,0:T(2,128)(2,1)S(1)} %copy.22, bf16[256,16,8,128]{3,2,1,0:T(8,128)(2,1)} %bitcast.68), kind=kOutput, calls=%fused_computation | convolution fusion | flops 8388608 | bytes 9502720 | tf_op jit(solution)/shard_map/bhl,blhd->bhd/dot_general | solution.py:35
  75.3 0.4 fusion.7
  75.6 0.3 convolution_convert_fusion.3
  76.0 23.1 %all_to_all.16 = bf16[16,16,1024]{2,1,0:T(8,128)(2,1)S(1)} all-to-all(bf16[16,16,1024]{2,1,0:T(8,128)(2,1)S(1)} %bitcast.73), channel_id=1, replica_groups=mesh['dp'=16,'tensor'=2] {'dp'}, dimensions={0} | all-to-all | bytes 1048576 | tf_op jit(solution)/shard_map/all_to_all | solution.py:87
  99.1 7.8 %fusion.5 = f32[256,4096]{1,0:T(8,128)} fusion(bf16[1024,4096]{1,0:T(8,128)(2,1)} %param.13, bf16[256,1024]{1,0:T(8,128)(2,1)S(1)} %bitcast.75, s32[256]{0:T(256)S(1)} %multiply_add_fusion, pred[256]{0:T(512)(128)(4,1)S(1)} %broadcast_compare_fusion), kind=kOutput, calls=%fused_computation.10 | convolution fusion | flops 2282094592 | bytes 13108480 | tf_op jit(solution)/shard_map/dot_general | solution.py:97
  106.9 0.0 copy-start
  107.0 0.0 reduce-scatter.2.cloned.1.call-update
  107.0 54.1 %reduce-scatter.2.cloned.1.call-done = f32[256,2048]{1,0:T(8,128)} async-done(((f32[256,4096]{1,0:T(8,128)}), f32[256,2048]{1,0:T(8,128)}) %reduce-scatter.2.cloned.1.call-update) | async-done | bytes 2097168 | tf_op jit(solution)/shard_map/reduce_scatter | solution.py:98
  161.1 0.0 copy-done
  161.1 2.8 %add_convert_fusion = bf16[256,2048]{1,0:T(8,128)(2,1)} fusion(f32[256,2048]{1,0:T(8,128)} %reduce-scatter.2.cloned.1.call-done, bf16[256,2048]{1,0:T(8,128)(2,1)S(1)} %copy-done), kind=kLoop, calls=%fused_computation.6 | loop fusion | flops 1572864 | bytes 4194304 | tf_op jit(solution)/shard_map/convert_element_type | solution.py:99
  (10 shorter events, 0.2 us)
Async XLA Ops:
  8.9 13.8 %all-to-all-start = ((s32[16,1,16]{2,1,0:T(1,128)}), s32[16,1,16]{2,1,0:T(1,128)S(1)}, u32[]{:S(2)}, u32[]{:S(2)}) async-start(s32[16,1,16]{2,1,0:T(1,128)} %sub.45), calls=%async_computation | async-start | bytes 16384 | tf_op jit(solution)/shard_map/all_to_all | solution.py:74
  22.7 35.5 %all-to-all-start.1 = ((bf16[16,16,3072]{2,1,0:T(8,128)(2,1)}), bf16[16,16,3072]{2,1,0:T(8,128)(2,1)S(1)}, u32[]{:S(2)}, u32[]{:S(2)}) async-start(bf16[16,16,3072]{2,1,0:T(8,128)(2,1)} %bitcast.1), calls=%async_computation.1 | async-start | bytes 3145728 | tf_op jit(solution)/shard_map/all_to_all | solution.py:73
  26.4 134.7 %reduce-scatter.2.cloned.1.call-start = ((), (), s32[]{:S(2)}) async-start(), calls=%async_computation.4 | async-start | bytes 6291456 | tf_op jit(solution)/shard_map/reduce_scatter | solution.py:98
  47.6 8.8 %copy-start.1 = (s32[256]{0:T(256)S(1)}, s32[256]{0:T(256)}, u32[]{:S(2)}) copy-start(s32[256]{0:T(256)} %param.12) | copy-start | bytes 3076
  106.9 54.1 %copy-start = (bf16[256,2048]{1,0:T(8,128)(2,1)S(1)}, bf16[256,2048]{1,0:T(8,128)(2,1)}, u32[]{:S(2)}) copy-start(bf16[256,2048]{1,0:T(8,128)(2,1)} %param.7) | copy-start | bytes 3145732
Sparse Core Ops, SparseCore 0:
  107.1 53.9 reduce-scatter.1
where the time goes:
time: 171 us
  waiting for transfers between devices  58.5 us (34%)
  local copies, waits for them, and re-layouts  34.9 us (20%)
  matrix products  24.1 us (14%)
  blocking collectives  23.1 us (14%)
  between operations  13.6 us (8%)
  starting transfers between devices  11.1 us (6%)
  other arithmetic  5.39 us (3%)
    reduce_scatter x1, waiting for transfers between devices, body(): lax.psum_scatter(partial_rows, 'tensor', scatter_dimension=1, tiled=True)  54.1 us
    all_to_all x1, blocking collectives, body(): lax.all_to_all(heads_rows.reshape(groups, capacity, width_here), 'dp', sp...  23.1 us
    unnamed x8, local copies, waits for them, and re-layouts  19.6 us
    slice x1, local copies, waits for them, and re-layouts, attend_local(): kv_cache[:, 1].reshape(streams_here, cache_len, heads_local, head_size)  12.4 us
    dot_general x1, matrix products, body(): jnp.dot(source_rows, w_out, preferred_element_type=jnp.float32)  7.83 us
    dot_general x1, matrix products, attend_local(): jnp.einsum('bhd,blhd->bhl', query, key_rows, preferred_element_type=jnp.f...  7.8 us
    all_to_all x1, starting transfers between devices, body(): lax.all_to_all(slot_ids, 'dp', split_axis=0, concat_axis=0, tiled=True)  7.39 us
    dot_general x1, matrix products, attend_local(): jnp.einsum('bhl,blhd->bhd', weights, value_rows, preferred_element_type=j...  5.69 us
  transfers between devices with their start and end apart: 3, of which 3 were waited for; matrix products, arithmetic and copies ran while one was open for 20% of the time, Pallas kernels for 0%

commit v1 on v0

--- a/solution.py
+++ b/solution.py
@@ -1,6 +1,10 @@
+import functools
+
 import jax
 import jax.numpy as jnp
 from jax import lax
+from jax.experimental import pallas as pl
+from jax.experimental.pallas import tpu as pltpu
 from jax.sharding import PartitionSpec as P
 
 HD = 128
@@ -39,7 +43,7 @@
     return mixed.astype(jnp.bfloat16).reshape(streams_here, heads_local * head_size)
 
 
-def body(residual, fresh_qkv, active, home_slot, kv_cache, lengths, w_out):
+def general_body(residual, fresh_qkv, active, home_slot, kv_cache, lengths, w_out):
     groups = lax.axis_size("dp")
     group_here = lax.axis_index("dp")
     streams_here = home_slot.shape[0]
@@ -99,6 +103,313 @@
     return (residual.astype(jnp.float32) + gained).astype(jnp.bfloat16)
 
 
+MESH = pl.DeviceIdType.MESH
+F32 = jnp.float32
+BF16 = jnp.bfloat16
+LANES = 128
+KV_PARTS = 4
+COLUMN_CHUNKS = 4
+
+
+def column_of(row, width):
+    return jnp.transpose(jnp.broadcast_to(row, (width, row.shape[1])))
+
+
+def iota(shape, dim):
+    return lax.broadcasted_iota(jnp.int32, shape, dim)
+
+
+def kernel(
+    n, heads, home_ref, active_ref, lengths_ref, fresh_ref, kv_hbm, w_hbm, residual_hbm,
+    out_ref,
+    kv, w, residual, send_q, got_q, send_a, got_a, owned, own, length_col, placing_t, mixed,
+    attended, part_send, part_got, kept,
+    kv_sem, w_sem, residual_sem, q_send_sem, q_got_sem, a_send_sem, a_got_sem, p_send_sem,
+    p_got_sem,
+):
+    me = lax.axis_index("dp")
+    side = lax.axis_index("tensor")
+    other = 1 - side
+    streams = home_ref.shape[1]
+    width = heads * HD
+    capacity = send_q.shape[1]
+    cache_len = kv.shape[2]
+    scale = HD ** -0.5
+    order = sorted(range(1, n), key=lambda k: abs(n - 2 * k))
+
+    barrier = pltpu.get_barrier_semaphore()
+    for k in order:
+        pl.semaphore_signal(
+            barrier, inc=1, device_id={"dp": lax.rem(me + k, n)}, device_id_type=MESH
+        )
+    pl.semaphore_signal(barrier, inc=1, device_id={"tensor": other}, device_id_type=MESH)
+
+    part = streams // KV_PARTS
+    kv_copies = [
+        pltpu.make_async_copy(
+            kv_hbm.at[pl.ds(i * part, part)], kv.at[pl.ds(i * part, part)], kv_sem.at[i]
+        )
+        for i in range(KV_PARTS)
+    ]
+    for copy in kv_copies:
+        copy.start()
+    w_copy = pltpu.make_async_copy(w_hbm, w, w_sem)
+    w_copy.start()
+    residual_copy = pltpu.make_async_copy(residual_hbm, residual, residual_sem)
+    residual_copy.start()
+
+    home = home_ref[...]
+    is_active = active_ref[...] > 0
+    shift = streams.bit_length() - 1
+    owner = jnp.where(is_active, lax.shift_right_logical(home, shift), -1).astype(F32)
+    local = ((home & (streams - 1)) + 1).astype(F32)
+    square = (streams, streams)
+    owner_cols = jnp.broadcast_to(owner, square)
+    same = (
+        (owner_cols == jnp.transpose(owner_cols))
+        & (owner_cols >= 0)
+        & (iota(square, 0) < iota(square, 1))
+    )
+    rank = jnp.sum(jnp.where(same, 1.0, 0.0), axis=0, keepdims=True)
+    target = jnp.where(owner >= 0, owner * capacity + rank, -1.0)
+    placing = jnp.where(iota(square, 0).astype(F32) == target, 1.0, 0.0)
+    placed = placing.astype(BF16)
+    ids = column_of(local, LANES).astype(BF16)
+    rows = jnp.dot(placed, fresh_ref[:, :width], preferred_element_type=F32).astype(BF16)
+    send_q[:, :, :width] = rows.reshape(n, capacity, width)
+    rows = jnp.dot(placed, ids, preferred_element_type=F32).astype(BF16)
+    send_q[:, :, width:] = rows.reshape(n, capacity, LANES)
+    placing_t[...] = jnp.transpose(placing).astype(BF16)
+    length_col[...] = column_of(lengths_ref[...].astype(F32), LANES)
+
+    pl.semaphore_wait(barrier, n)
+
+    def exchange(source, landing, send_sem, got_sem):
+        copies = []
+        for k in order:
+            peer = lax.rem(me + k, n)
+            copies.append(
+                pltpu.make_async_remote_copy(
+                    src_ref=source.at[peer],
+                    dst_ref=landing.at[me],
+                    send_sem=send_sem.at[k],
+                    recv_sem=got_sem.at[k],
+                    device_id={"dp": peer},
+                    device_id_type=MESH,
+                )
+            )
+        for copy in copies:
+            copy.start()
+        return copies
+
+    copies = exchange(send_q, got_q, q_send_sem, q_got_sem)
+    own_block = pltpu.make_async_copy(send_q.at[me], got_q.at[me], q_got_sem.at[0])
+    own_block.start()
+    lane = iota((streams, LANES), 1)
+    own_scores = jnp.zeros((streams, LANES), F32)
+    for h in range(heads):
+        query = fresh_ref[:, h * HD : (h + 1) * HD].astype(F32)
+        key = fresh_ref[:, width + h * HD : width + (h + 1) * HD].astype(F32)
+        own_h = jnp.sum(query * key, axis=1, keepdims=True) * scale
+        own_scores = jnp.where(lane == h, own_h, own_scores)
+    own[...] = own_scores
+    own_block.wait()
+    for copy in copies:
+        copy.wait()
+
+    got_ids = got_q[:, :, width:].reshape(n * capacity, LANES)[:, :1].astype(F32) - 1.0
+    matched_t = jnp.where(iota(square, 1).astype(F32) == got_ids, 1.0, 0.0)
+    matched = jnp.transpose(matched_t).astype(BF16)
+    owned[...] = jnp.dot(
+        matched, got_q[:, :, :width].reshape(n * capacity, width), preferred_element_type=F32
+    ).astype(BF16)
+    matched_t = matched_t.astype(BF16)
+    for copy in kv_copies:
+        copy.wait()
+
+    batch = 16
+    spread = (batch, batch * cache_len)
+    in_slot = iota(spread, 1) // cache_len == iota(spread, 0)
+    position = lax.rem(iota(spread, 1), cache_len).astype(F32)
+    small_lane = iota((batch, LANES), 1)
+
+    def attend(step, carry):
+        slots = pl.ds(pl.multiple_of(step * batch, batch), batch)
+        queries = owned[slots, :]
+        valid = in_slot & (position < length_col[slots, :1])
+        sums = jnp.zeros((batch, LANES), F32)
+        for h in range(heads):
+            span = slice(h * HD, (h + 1) * HD)
+            keys = kv[slots, 0, :, span].reshape(batch * cache_len, HD)
+            values = kv[slots, 1, :, span].reshape(batch * cache_len, HD)
+            scores = (
+                lax.dot_general(
+                    queries[:, span], keys, (((1,), (1,)), ((), ())), preferred_element_type=F32
+                )
+                * scale
+            )
+            scores = jnp.where(valid, scores, -1e30)
+            top = jnp.max(scores, axis=1, keepdims=True)
+            raw = jnp.exp(scores - top)
+            total = jnp.sum(raw, axis=1, keepdims=True)
+            weights = (raw / total).astype(BF16)
+            mixed[slots, span] = jnp.dot(weights, values, preferred_element_type=F32).astype(BF16)
+            here = (lax.rem(small_lane, heads) == h) & (small_lane < 3 * heads)
+            sums = jnp.where(here, top + jnp.log(total), sums)
+        first = sums.astype(BF16).astype(F32)
+        second = (sums - first).astype(BF16).astype(F32)
+        third = sums - first - second
+        digits = jnp.where(
+            small_lane < heads, first, jnp.where(small_lane < 2 * heads, second, third)
+        )
+        digits = jnp.where(small_lane == 3 * heads, 1.0, digits)
+        mixed[slots, width:] = digits.astype(BF16)
+        return carry
+
+    lax.fori_loop(0, streams // batch, attend, 0)
+
+    back = jnp.dot(matched_t, mixed[...], preferred_element_type=F32).astype(BF16)
+    send_a[...] = back.reshape(n, capacity, width + LANES)
+    copies = exchange(send_a, got_a, a_send_sem, a_got_sem)
+    own_block = pltpu.make_async_copy(send_a.at[me], got_a.at[me], a_got_sem.at[0])
+    own_block.start()
+    w_copy.wait()
+    residual_copy.wait()
+    own_block.wait()
+    for copy in copies:
+        copy.wait()
+
+    place_back = placing_t[...]
+    extra = jnp.dot(
+        place_back,
+        got_a[:, :, width:].reshape(n * capacity, LANES),
+        preferred_element_type=F32,
+    )
+    flag = extra[:, 3 * heads : 3 * heads + 1]
+    own_scores = own[...]
+    for h in range(heads):
+        span = slice(h * HD, (h + 1) * HD)
+        cached = jnp.dot(
+            place_back,
+            got_a[:, :, span].reshape(n * capacity, HD),
+            preferred_element_type=F32,
+        )
+        lse = (
+            extra[:, h : h + 1]
+            + extra[:, heads + h : heads + h + 1]
+            + extra[:, 2 * heads + h : 2 * heads + h + 1]
+        )
+        own_h = own_scores[:, h : h + 1]
+        top = jnp.maximum(lse, own_h)
+        from_cache = jnp.exp(lse - top)
+        from_own = jnp.exp(own_h - top)
+        share = flag / (from_cache + from_own)
+        value = fresh_ref[:, 2 * width + h * HD : 2 * width + (h + 1) * HD].astype(F32)
+        attended[:, span] = (
+            (from_cache * share) * cached + (from_own * share) * value
+        ).astype(BF16)
+
+    columns = residual.shape[1]
+    chunk = columns // COLUMN_CHUNKS
+    sends = []
+    for c in range(COLUMN_CHUNKS):
+        span = pl.ds(pl.multiple_of(other * columns + c * chunk, LANES), chunk)
+        part_send[c] = jnp.dot(
+            attended[...], w[:, span], preferred_element_type=F32
+        ).astype(BF16)
+        copy = pltpu.make_async_remote_copy(
+            src_ref=part_send.at[c],
+            dst_ref=part_got.at[c],
+            send_sem=p_send_sem.at[c],
+            recv_sem=p_got_sem.at[c],
+            device_id={"tensor": other},
+            device_id_type=MESH,
+        )
+        copy.start()
+        sends.append(copy)
+    for c in range(COLUMN_CHUNKS):
+        span = pl.ds(pl.multiple_of(side * columns + c * chunk, LANES), chunk)
+        kept[c] = residual[:, c * chunk : (c + 1) * chunk].astype(F32) + jnp.dot(
+            attended[...], w[:, span], preferred_element_type=F32
+        )
+    for c in range(COLUMN_CHUNKS):
+        sends[c].wait()
+        out_ref[:, c * chunk : (c + 1) * chunk] = (
+            kept[c] + part_got[c].astype(F32)
+        ).astype(BF16)
+
+
+def fused_body(residual, fresh_qkv, active, home_slot, kv_cache, lengths, w_out):
+    n = lax.axis_size("dp")
+    streams, columns = residual.shape
+    width = fresh_qkv.shape[2]
+    heads = width // HD
+    capacity = streams // n
+    row = (n, capacity, width + LANES)
+    chunk = columns // COLUMN_CHUNKS
+    vmem = pl.BlockSpec(memory_space=pltpu.VMEM)
+    anywhere = pl.BlockSpec(memory_space=pl.ANY)
+    dma = pltpu.SemaphoreType.DMA
+    return pl.pallas_call(
+        functools.partial(kernel, n, heads),
+        out_shape=jax.ShapeDtypeStruct((streams, columns), BF16),
+        in_specs=[vmem] * 4 + [anywhere] * 3,
+        out_specs=vmem,
+        scratch_shapes=[
+            pltpu.VMEM(kv_cache.shape, BF16),
+            pltpu.VMEM(w_out.shape, BF16),
+            pltpu.VMEM(residual.shape, BF16),
+            pltpu.VMEM(row, BF16),
+            pltpu.VMEM(row, BF16),
+            pltpu.VMEM(row, BF16),
+            pltpu.VMEM(row, BF16),
+            pltpu.VMEM((streams, width), BF16),
+            pltpu.VMEM((streams, LANES), F32),
+            pltpu.VMEM((streams, LANES), F32),
+            pltpu.VMEM((streams, streams), BF16),
+            pltpu.VMEM((streams, width + LANES), BF16),
+            pltpu.VMEM((streams, width), BF16),
+            pltpu.VMEM((COLUMN_CHUNKS, streams, chunk), BF16),
+            pltpu.VMEM((COLUMN_CHUNKS, streams, chunk), BF16),
+            pltpu.VMEM((COLUMN_CHUNKS, streams, chunk), F32),
+            dma((KV_PARTS,)),
+            dma,
+            dma,
+            dma((n,)),
+            dma((n,)),
+            dma((n,)),
+            dma((n,)),
+            dma((COLUMN_CHUNKS,)),
+            dma((COLUMN_CHUNKS,)),
+        ],
+        compiler_params=pltpu.CompilerParams(
+            collective_id=0, has_side_effects=True, vmem_limit_bytes=60 * 1024 * 1024
+        ),
+    )(
+        home_slot.reshape(1, streams),
+        active.reshape(1, streams),
+        lengths.reshape(1, streams),
+        fresh_qkv.reshape(streams, 3 * width),
+        kv_cache,
+        w_out,
+        residual,
+    )
+
+
+def body(residual, fresh_qkv, active, home_slot, kv_cache, lengths, w_out):
+    n = lax.axis_size("dp")
+    streams = home_slot.shape[0]
+    fits = (
+        lax.axis_size("tensor") == 2
+        and streams % n == 0
+        and (streams // n) % 16 == 0
+        and streams <= 256
+        and streams & (streams - 1) == 0
+    )
+    chosen = fused_body if fits else general_body
+    return chosen(residual, fresh_qkv, active, home_slot, kv_cache, lengths, w_out)
+
+
 def solution(mesh):
     placed = (
         P("dp", "tensor"),

time: 171 us -> 112 us (0.65)
  Pallas kernels: 0 us -> 106 us
  waiting for transfers between devices: 58.5 us -> 0 us
  local copies, waits for them, and re-layouts: 34.9 us -> 5.77 us
  matrix products: 24.1 us -> 0 us
  blocking collectives: 23.1 us -> 0 us
  between operations: 13.6 us -> 0.02 us
  starting transfers between devices: 11.1 us -> 0 us
  other arithmetic: 5.39 us -> 0 us
    pallas_call x0 -> x1, Pallas kernels: none -> 106 us  [fused_body(): pl.pallas_call(functools.partial(kernel, n, heads), out_shape=jax.ShapeDt...]
    reduce_scatter x1 -> x0, waiting for transfers between devices: 54.1 us -> none  [body(): lax.psum_scatter(partial_rows, 'tensor', scatter_dimension=1, tiled=True)]
    dot_general x6 -> x0, matrix products: 24.1 us -> none  [the longest x1 7.83 us: body(): jnp.dot(source_rows, w_out, preferred_element_type=jnp.float32)]
    all_to_all x1 -> x0, blocking collectives: 23.1 us -> none  [body(): lax.all_to_all(heads_rows.reshape(groups, capacity, width_here), 'dp', sp...]
    unnamed x8 -> x2, local copies, waits for them, and re-layouts: 19.6 us -> 4.01 us
    slice x1 -> x0, local copies, waits for them, and re-layouts: 12.4 us -> none  [attend_local(): kv_cache[:, 1].reshape(streams_here, cache_len, heads_local, head_size)]
    all_to_all x2 -> x0, starting transfers between devices: 11.1 us -> none  [the longest x1 7.39 us: body(): lax.all_to_all(slot_ids, 'dp', split_axis=0, concat_axis=0, tiled=True)]
    all_to_all x2 -> x0, waiting for transfers between devices: 4.43 us -> none  [the longest x1 2.8 us: body(): lax.all_to_all(slot_ids, 'dp', split_axis=0, concat_axis=0, tiled=True)]
  transfers between devices with their start and end apart: 3 -> 0, of which waited for: 3 -> 0; matrix products, arithmetic and copies ran while one was open for 20% -> 0% of each run, Pallas kernels for 0% -> 0%
where the time goes in v1:
time: 112 us
  Pallas kernels  106 us (95%)
  local copies, waits for them, and re-layouts  5.77 us (5%)
    pallas_call x1, Pallas kernels, fused_body(): pl.pallas_call(functools.partial(kernel, n, heads), out_shape=jax.ShapeDt...  106 us
    unnamed x2, local copies, waits for them, and re-layouts  4.01 us

profile of v1, /device:TPU:0, one launch (start us, length us, event | category | flops | bytes accessed | tf_op | source)
XLA Modules:
  0.0 111.5 jit_solution(3454924135009762546)
XLA Ops:
  0.0 1.7 %copy.9 = bf16[256,3,1024]{0,2,1:T(8,128)(2,1)S(1)} copy(bf16[256,3,1024]{2,0,1:T(8,128)(2,1)} %param.8) | data formatting | bytes 3145728 | tf_op args[1]
  1.7 1.8 %copy.10.fresh_ref = bf16[256,3072]{1,0:T(8,128)(2,1)} copy(bf16[256,3072]{0,1:T(8,128)(2,1)S(1)} %bitcast.4) | data formatting | bytes 3145728 | tf_op jit(solution)/shard_map/reshape | solution.py:392
  3.5 105.8 %shard_map.73 = bf16[256,2048]{1,0:T(8,128)(2,1)} custom-call(s32[1,256]{1,0:T(1,128)} %bitcast.5, s32[1,256]{1,0:T(1,128)} %bitcast.6, s32[1,256]{1,0:T(1,128)} %bitcast.7, bf16[256,3072]{1,0:T(8,128)(2,1)} %copy.10.fresh_ref, bf16[256,2,16,1024]{3,2,1,0:T(8,128)(2,1)} %kv_hbm.1, bf16[1024,4096]{1,0:T(8,128)(2,1)} %w_hbm.1, bf16[256,2048]{1,0:T(8,128)(2,1)} %residual_hbm.1), custom_call_target="tpu_custom_call" | custom-call | tf_op jit(solution)/shard_map/pallas_call | solution.py:353
  109.2 2.3 %copy.12 = bf16[256,2048]{1,0:T(8,128)(2,1)} copy(bf16[256,2048]{1,0:T(8,128)(2,1)} %shard_map.73) | data formatting | bytes 2097152

commit v2 on v1

--- a/solution.py
+++ b/solution.py
@@ -109,10 +109,20 @@
 LANES = 128
 KV_PARTS = 4
 COLUMN_CHUNKS = 4
+ROW_GROUPS = 4
+GROUP_ORDER = (0, 2, 1, 3)
 
 
 def column_of(row, width):
     return jnp.transpose(jnp.broadcast_to(row, (width, row.shape[1])))
+
+
+def partner_of(me, k, n):
+    peer = me
+    for bit in range(n.bit_length() - 1):
+        if k >> bit & 1:
+            peer = peer + (1 - 2 * lax.rem(me // (1 << bit), 2)) * (1 << bit)
+    return peer
 
 
 def iota(shape, dim):
@@ -123,7 +133,7 @@
     n, heads, home_ref, active_ref, lengths_ref, fresh_ref, kv_hbm, w_hbm, residual_hbm,
     out_ref,
     kv, w, residual, send_q, got_q, send_a, got_a, owned, own, length_col, placing_t, mixed,
-    attended, part_send, part_got, kept,
+    key_rows, value_rows, attended, part_send, part_got, kept, gained,
     kv_sem, w_sem, residual_sem, q_send_sem, q_got_sem, a_send_sem, a_got_sem, p_send_sem,
     p_got_sem,
 ):
@@ -135,12 +145,13 @@
     capacity = send_q.shape[1]
     cache_len = kv.shape[2]
     scale = HD ** -0.5
-    order = sorted(range(1, n), key=lambda k: abs(n - 2 * k))
+    order = list(range(n // 2, n)) + list(range(n // 4, n // 2)) + list(range(1, n // 4))
+    peers = [partner_of(me, k, n) for k in range(n)]
 
     barrier = pltpu.get_barrier_semaphore()
     for k in order:
         pl.semaphore_signal(
-            barrier, inc=1, device_id={"dp": lax.rem(me + k, n)}, device_id_type=MESH
+            barrier, inc=1, device_id={"dp": peers[k]}, device_id_type=MESH
         )
     pl.semaphore_signal(barrier, inc=1, device_id={"tensor": other}, device_id_type=MESH)
 
@@ -185,35 +196,39 @@
     pl.semaphore_wait(barrier, n)
 
     def exchange(source, landing, send_sem, got_sem):
-        copies = []
+        copies = [pltpu.make_async_copy(source.at[me], landing.at[me], got_sem.at[0])]
+        copies[0].start()
+        by_order = {}
         for k in order:
-            peer = lax.rem(me + k, n)
-            copies.append(
-                pltpu.make_async_remote_copy(
-                    src_ref=source.at[peer],
-                    dst_ref=landing.at[me],
-                    send_sem=send_sem.at[k],
-                    recv_sem=got_sem.at[k],
-                    device_id={"dp": peer},
-                    device_id_type=MESH,
-                )
+            by_order[k] = pltpu.make_async_remote_copy(
+                src_ref=source.at[peers[k]],
+                dst_ref=landing.at[me],
+                send_sem=send_sem.at[k],
+                recv_sem=got_sem.at[k],
+                device_id={"dp": peers[k]},
+                device_id_type=MESH,
             )
-        for copy in copies:
-            copy.start()
-        return copies
+            by_order[k].start()
+        return copies + [by_order[k] for k in range(1, n)]
 
     copies = exchange(send_q, got_q, q_send_sem, q_got_sem)
-    own_block = pltpu.make_async_copy(send_q.at[me], got_q.at[me], q_got_sem.at[0])
-    own_block.start()
+    key_rows[...] = jnp.dot(
+        placed, fresh_ref[:, width : 2 * width], preferred_element_type=F32
+    ).astype(BF16)
+    value_rows[...] = (
+        jnp.dot(placed, fresh_ref[:, 2 * width :], preferred_element_type=F32)
+        .astype(BF16)
+        .reshape(n, capacity, width)
+    )
     lane = iota((streams, LANES), 1)
     own_scores = jnp.zeros((streams, LANES), F32)
     for h in range(heads):
-        query = fresh_ref[:, h * HD : (h + 1) * HD].astype(F32)
-        key = fresh_ref[:, width + h * HD : width + (h + 1) * HD].astype(F32)
+        span = slice(h * HD, (h + 1) * HD)
+        query = send_q[:, :, span].reshape(streams, HD).astype(F32)
+        key = key_rows[:, span].astype(F32)
         own_h = jnp.sum(query * key, axis=1, keepdims=True) * scale
         own_scores = jnp.where(lane == h, own_h, own_scores)
-    own[...] = own_scores
-    own_block.wait()
+    own[...] = own_scores.reshape(n, capacity, LANES)
     for copy in copies:
         copy.wait()
 
@@ -228,41 +243,50 @@
         copy.wait()
 
     batch = 16
-    spread = (batch, batch * cache_len)
-    in_slot = iota(spread, 1) // cache_len == iota(spread, 0)
+    spread = (heads * batch, batch * cache_len)
+    in_slot = iota(spread, 1) // cache_len == lax.rem(iota(spread, 0), batch)
     position = lax.rem(iota(spread, 1), cache_len).astype(F32)
     small_lane = iota((batch, LANES), 1)
 
     def attend(step, carry):
         slots = pl.ds(pl.multiple_of(step * batch, batch), batch)
-        queries = owned[slots, :]
-        valid = in_slot & (position < length_col[slots, :1])
+        spans = [slice(h * HD, (h + 1) * HD) for h in range(heads)]
+        lens = jnp.concatenate([length_col[slots, :]] * heads, axis=0)[:, :1]
+        valid = in_slot & (position < lens)
+        scores = jnp.concatenate(
+            [
+                lax.dot_general(
+                    owned[slots, span],
+                    kv[slots, 0, :, span].reshape(batch * cache_len, HD),
+                    (((1,), (1,)), ((), ())),
+                    preferred_element_type=F32,
+                )
+                for span in spans
+            ],
+            axis=0,
+        )
+        scores = jnp.where(valid, scores * scale, -1e30)
+        top = jnp.max(scores, axis=1, keepdims=True)
+        raw = jnp.exp(scores - top)
+        total = jnp.sum(raw, axis=1, keepdims=True)
+        weights = (raw / total).astype(BF16)
+        lse = top + jnp.log(total)
         sums = jnp.zeros((batch, LANES), F32)
-        for h in range(heads):
-            span = slice(h * HD, (h + 1) * HD)
-            keys = kv[slots, 0, :, span].reshape(batch * cache_len, HD)
-            values = kv[slots, 1, :, span].reshape(batch * cache_len, HD)
-            scores = (
-                lax.dot_general(
-                    queries[:, span], keys, (((1,), (1,)), ((), ())), preferred_element_type=F32
-                )
-                * scale
-            )
-            scores = jnp.where(valid, scores, -1e30)
-            top = jnp.max(scores, axis=1, keepdims=True)
-            raw = jnp.exp(scores - top)
-            total = jnp.sum(raw, axis=1, keepdims=True)
-            weights = (raw / total).astype(BF16)
-            mixed[slots, span] = jnp.dot(weights, values, preferred_element_type=F32).astype(BF16)
+        for h, span in enumerate(spans):
+            rows = slice(h * batch, (h + 1) * batch)
+            mixed[slots, span] = jnp.dot(
+                weights[rows],
+                kv[slots, 1, :, span].reshape(batch * cache_len, HD),
+                preferred_element_type=F32,
+            ).astype(BF16)
             here = (lax.rem(small_lane, heads) == h) & (small_lane < 3 * heads)
-            sums = jnp.where(here, top + jnp.log(total), sums)
+            sums = jnp.where(here, lse[rows], sums)
         first = sums.astype(BF16).astype(F32)
         second = (sums - first).astype(BF16).astype(F32)
         third = sums - first - second
         digits = jnp.where(
             small_lane < heads, first, jnp.where(small_lane < 2 * heads, second, third)
         )
-        digits = jnp.where(small_lane == 3 * heads, 1.0, digits)
         mixed[slots, width:] = digits.astype(BF16)
         return carry
 
@@ -271,71 +295,80 @@
     back = jnp.dot(matched_t, mixed[...], preferred_element_type=F32).astype(BF16)
     send_a[...] = back.reshape(n, capacity, width + LANES)
     copies = exchange(send_a, got_a, a_send_sem, a_got_sem)
-    own_block = pltpu.make_async_copy(send_a.at[me], got_a.at[me], a_got_sem.at[0])
-    own_block.start()
     w_copy.wait()
     residual_copy.wait()
-    own_block.wait()
-    for copy in copies:
-        copy.wait()
-
-    place_back = placing_t[...]
-    extra = jnp.dot(
-        place_back,
-        got_a[:, :, width:].reshape(n * capacity, LANES),
-        preferred_element_type=F32,
-    )
-    flag = extra[:, 3 * heads : 3 * heads + 1]
-    own_scores = own[...]
-    for h in range(heads):
-        span = slice(h * HD, (h + 1) * HD)
-        cached = jnp.dot(
-            place_back,
-            got_a[:, :, span].reshape(n * capacity, HD),
-            preferred_element_type=F32,
-        )
-        lse = (
-            extra[:, h : h + 1]
-            + extra[:, heads + h : heads + h + 1]
-            + extra[:, 2 * heads + h : 2 * heads + h + 1]
-        )
-        own_h = own_scores[:, h : h + 1]
-        top = jnp.maximum(lse, own_h)
-        from_cache = jnp.exp(lse - top)
-        from_own = jnp.exp(own_h - top)
-        share = flag / (from_cache + from_own)
-        value = fresh_ref[:, 2 * width + h * HD : 2 * width + (h + 1) * HD].astype(F32)
-        attended[:, span] = (
-            (from_cache * share) * cached + (from_own * share) * value
-        ).astype(BF16)
 
     columns = residual.shape[1]
-    chunk = columns // COLUMN_CHUNKS
+    step = columns // COLUMN_CHUNKS
+    members = n // ROW_GROUPS
     sends = []
-    for c in range(COLUMN_CHUNKS):
-        span = pl.ds(pl.multiple_of(other * columns + c * chunk, LANES), chunk)
-        part_send[c] = jnp.dot(
-            attended[...], w[:, span], preferred_element_type=F32
-        ).astype(BF16)
+    for g, first_k in enumerate(GROUP_ORDER):
+        group = range(first_k * members, (first_k + 1) * members)
+        for k in group:
+            if k:
+                copies[k].wait_recv()
+            else:
+                copies[k].wait()
+        arrived = jnp.concatenate([got_a[peers[k]] for k in group], axis=0).astype(F32)
+        own_rows = jnp.concatenate([own[peers[k]] for k in group], axis=0)
+        values = jnp.concatenate([value_rows[peers[k]] for k in group], axis=0).astype(F32)
+        for h in range(heads):
+            span = slice(h * HD, (h + 1) * HD)
+            at = width + h
+            lse = (
+                arrived[:, at : at + 1]
+                + arrived[:, at + heads : at + heads + 1]
+                + arrived[:, at + 2 * heads : at + 2 * heads + 1]
+            )
+            own_h = own_rows[:, h : h + 1]
+            top = jnp.maximum(lse, own_h)
+            from_cache = jnp.exp(lse - top)
+            from_own = jnp.exp(own_h - top)
+            share = 1.0 / (from_cache + from_own)
+            attended[g, :, span] = (
+                (from_cache * share) * arrived[:, span] + (from_own * share) * values[:, span]
+            ).astype(BF16)
+        for c in range(COLUMN_CHUNKS):
+            here = pl.ds(pl.multiple_of(other * columns + c * step, LANES), step)
+            part_send[g, :, c * step : (c + 1) * step] = jnp.dot(
+                attended[g], w[:, here], preferred_element_type=F32
+            ).astype(BF16)
         copy = pltpu.make_async_remote_copy(
-            src_ref=part_send.at[c],
-            dst_ref=part_got.at[c],
-            send_sem=p_send_sem.at[c],
-            recv_sem=p_got_sem.at[c],
+            src_ref=part_send.at[g],
+            dst_ref=part_got.at[g],
+            send_sem=p_send_sem.at[g],
+            recv_sem=p_got_sem.at[g],
             device_id={"tensor": other},
             device_id_type=MESH,
         )
         copy.start()
         sends.append(copy)
+        for c in range(COLUMN_CHUNKS):
+            here = pl.ds(pl.multiple_of(side * columns + c * step, LANES), step)
+            kept[g, :, c * step : (c + 1) * step] = jnp.dot(
+                attended[g], w[:, here], preferred_element_type=F32
+            )
+    for k in range(1, n):
+        copies[k].wait_send()
+    for g, first_k in enumerate(GROUP_ORDER):
+        sends[g].wait()
+        total = kept[g] + part_got[g].astype(F32)
+        high = total.astype(BF16)
+        low = (total - high.astype(F32)).astype(BF16)
+        for i in range(members):
+            block = peers[first_k * members + i]
+            rows = slice(i * capacity, (i + 1) * capacity)
+            gained[0, block] = high[rows]
+            gained[1, block] = low[rows]
+    place_back = placing_t[...]
     for c in range(COLUMN_CHUNKS):
-        span = pl.ds(pl.multiple_of(side * columns + c * chunk, LANES), chunk)
-        kept[c] = residual[:, c * chunk : (c + 1) * chunk].astype(F32) + jnp.dot(
-            attended[...], w[:, span], preferred_element_type=F32
-        )
-    for c in range(COLUMN_CHUNKS):
-        sends[c].wait()
-        out_ref[:, c * chunk : (c + 1) * chunk] = (
-            kept[c] + part_got[c].astype(F32)
+        span = slice(c * step, (c + 1) * step)
+        high = gained[0, :, :, span].reshape(streams, step)
+        low = gained[1, :, :, span].reshape(streams, step)
+        out_ref[:, span] = (
+            residual[:, span].astype(F32)
+            + jnp.dot(place_back, high, preferred_element_type=F32)
+            + jnp.dot(place_back, low, preferred_element_type=F32)
         ).astype(BF16)
 
 
@@ -346,7 +379,7 @@
     heads = width // HD
     capacity = streams // n
     row = (n, capacity, width + LANES)
-    chunk = columns // COLUMN_CHUNKS
+    rows = streams // ROW_GROUPS
     vmem = pl.BlockSpec(memory_space=pltpu.VMEM)
     anywhere = pl.BlockSpec(memory_space=pl.ANY)
     dma = pltpu.SemaphoreType.DMA
@@ -364,14 +397,17 @@
             pltpu.VMEM(row, BF16),
             pltpu.VMEM(row, BF16),
             pltpu.VMEM((streams, width), BF16),
-            pltpu.VMEM((streams, LANES), F32),
+            pltpu.VMEM((n, capacity, LANES), F32),
             pltpu.VMEM((streams, LANES), F32),
             pltpu.VMEM((streams, streams), BF16),
             pltpu.VMEM((streams, width + LANES), BF16),
             pltpu.VMEM((streams, width), BF16),
-            pltpu.VMEM((COLUMN_CHUNKS, streams, chunk), BF16),
-            pltpu.VMEM((COLUMN_CHUNKS, streams, chunk), BF16),
-            pltpu.VMEM((COLUMN_CHUNKS, streams, chunk), F32),
+            pltpu.VMEM((n, capacity, width), BF16),
+            pltpu.VMEM((ROW_GROUPS, rows, width), BF16),
+            pltpu.VMEM((ROW_GROUPS, rows, columns), BF16),
+            pltpu.VMEM((ROW_GROUPS, rows, columns), BF16),
+            pltpu.VMEM((ROW_GROUPS, rows, columns), F32),
+            pltpu.VMEM((2, n, capacity, columns), BF16),
             dma((KV_PARTS,)),
             dma,
             dma,
@@ -379,8 +415,8 @@
             dma((n,)),
             dma((n,)),
             dma((n,)),
-            dma((COLUMN_CHUNKS,)),
-            dma((COLUMN_CHUNKS,)),
+            dma((ROW_GROUPS,)),
+            dma((ROW_GROUPS,)),
         ],
         compiler_params=pltpu.CompilerParams(
             collective_id=0, has_side_effects=True, vmem_limit_bytes=60 * 1024 * 1024
@@ -401,6 +437,8 @@
     streams = home_slot.shape[0]
     fits = (
         lax.axis_size("tensor") == 2
+        and n % ROW_GROUPS == 0
+        and n & (n - 1) == 0
         and streams % n == 0
         and (streams // n) % 16 == 0
         and streams <= 256

time: 112 us -> 70.9 us (0.63)
  Pallas kernels: 106 us -> 64.9 us
    pallas_call x1, Pallas kernels: 106 us -> 64.9 us  [fused_body(): pl.pallas_call(functools.partial(kernel, n, heads), out_shape=jax.ShapeDt...]
where the time goes in v2:
time: 70.9 us; the launch traced here: 70.7 us
  Pallas kernels  64.9 us (92%)
  local copies, waits for them, and re-layouts  5.77 us (8%)
    pallas_call x1, Pallas kernels, fused_body(): pl.pallas_call(functools.partial(kernel, n, heads), out_shape=jax.ShapeDt...  64.9 us
    unnamed x2, local copies, waits for them, and re-layouts  4.01 us
    reshape x1, local copies, waits for them, and re-layouts, fused_body(): fresh_qkv.reshape(streams, 3 * width)  1.76 us

profile of v2, /device:TPU:0, one launch (start us, length us, event | category | flops | bytes accessed | tf_op | source)
XLA Modules:
  0.0 70.7 jit_solution(10960119809885361429)
XLA Ops:
  0.0 1.7 %copy.9 = bf16[256,3,1024]{0,2,1:T(8,128)(2,1)S(1)} copy(bf16[256,3,1024]{2,0,1:T(8,128)(2,1)} %param.8) | data formatting | bytes 3145728 | tf_op args[1]
  1.7 1.8 %copy.10.fresh_ref = bf16[256,3072]{1,0:T(8,128)(2,1)} copy(bf16[256,3072]{0,1:T(8,128)(2,1)S(1)} %bitcast.4) | data formatting | bytes 3145728 | tf_op jit(solution)/shard_map/reshape | solution.py:428
  3.5 64.9 %shard_map.73 = bf16[256,2048]{1,0:T(8,128)(2,1)} custom-call(s32[1,256]{1,0:T(1,128)} %bitcast.5, s32[1,256]{1,0:T(1,128)} %bitcast.6, s32[1,256]{1,0:T(1,128)} %bitcast.7, bf16[256,3072]{1,0:T(8,128)(2,1)} %copy.10.fresh_ref, bf16[256,2,16,1024]{3,2,1,0:T(8,128)(2,1)} %kv_hbm.1, bf16[1024,4096]{1,0:T(8,128)(2,1)} %w_hbm.1, bf16[256,2048]{1,0:T(8,128)(2,1)} %residual_hbm.1), custom_call_target="tpu_custom_call" | custom-call | tf_op jit(solution)/shard_map/pallas_call | solution.py:386
  68.4 2.3 %copy.12 = bf16[256,2048]{1,0:T(8,128)(2,1)} copy(bf16[256,2048]{1,0:T(8,128)(2,1)} %shard_map.73) | data formatting | bytes 2097152
